TPU v7x, 32 devices: a whole 2x2x4 slice. The times are simulated.
32 devices in a mesh: blk: 16 (over z, x, core), rep: 2 (over y).
Axes of the slice: x: 2, y: 2, z: 4, core: 2. Of those that a mesh axis runs over, the one named last changes fastest.
Arguments:
- particles: bfloat16 [896, 2048], P(('blk', 'rep')), may hold values from -0.0029907227 to 0.0029907227
- scores: bfloat16 [896, 2048], P(('blk', 'rep')), may hold values from -60 to 60, as said below
- spread: float32 [1], replicated, may hold values from 0.00034816 to 0.00069632
Outputs:
- direction: float32 [896, 2048], P(('blk', 'rep'))
Inputs may be any that keep to these rules, and one draw needn't show every extreme that they name: `scores`: scores of the particles' log posterior.
All inputs are finite; a program needn't handle non-finite values.
Results may differ from a plain program's by a relative error of at most 0.0003.
Values may be sent and summed in bfloat16 or wider, within the bound.
A program may use at most 128 MiB of HBM per device.

v0:
```python
import jax
import jax.numpy as jnp
from jax import lax
from jax.sharding import PartitionSpec as P


def kernel_weights(targets, target_norm, source_x, inverse):
    cross_dots = lax.dot_general(
        targets, source_x, (((1,), (1,)), ((), ())), preferred_element_type=jnp.float32
    )
    source_wide = source_x.astype(jnp.float32)
    source_norm = jnp.sum(source_wide * source_wide, axis=1)
    squared = jnp.maximum(target_norm[:, None] + source_norm[None, :] - 2.0 * cross_dots, 0.0)
    return jnp.exp(-squared * inverse)


def shards(particles, scores, spread):
    inverse = 1.0 / spread[0]
    own_count = particles.shape[0]
    population = own_count * lax.axis_size("blk") * lax.axis_size("rep")
    targets = lax.all_gather(particles, "rep", axis=0, tiled=True)
    target_wide = targets.astype(jnp.float32)
    target_norm = jnp.sum(target_wide * target_wide, axis=1)
    stacked = jnp.stack([scores, particles], axis=0)
    source = lax.all_gather(stacked, "blk", axis=1, tiled=True)
    weights = kernel_weights(targets, target_norm, source[1], inverse)
    weights_low = weights.astype(jnp.bfloat16)
    combined_step = jnp.einsum(
        "ij,cjd->cid", weights_low, source, preferred_element_type=jnp.float32
    )
    row_total = jnp.sum(weights, axis=1)
    drive_sum = combined_step[0]
    pull_sum = combined_step[1]
    partial_value = (
        drive_sum + 2.0 * inverse * (target_wide * row_total[:, None] - pull_sum)
    ) / population
    return lax.psum_scatter(partial_value, "rep", scatter_dimension=0, tiled=True)


def solution(mesh):
    return jax.shard_map(
        shards,
        mesh=mesh,
        in_specs=(P(("blk", "rep"), None), P(("blk", "rep"), None), P()),
        out_specs=P(("blk", "rep"), None),
        check_vma=False,
    )
```

profile of v0, /device:TPU:0, one launch (start us, length us, event | category | flops | bytes accessed | tf_op | source)
XLA Modules:
  0.0 90.4 jit_solution(13617939061221818914)
XLA Ops:
  6.5 0.0 all-gather.3.cloned.1.call-start
  6.5 1.0 %pad_maximum_fusion = bf16[2,28,2048]{2,1,0:T(8,128)(2,1)S(1)} fusion(bf16[1,28,2048]{2,1,0:T(8,128)(2,1)} %bitcast.53, bf16[1,28,2048]{2,1,0:T(8,128)(2,1)} %bitcast.55), kind=kLoop, calls=%fused_computation.20 | loop fusion | flops 114688 | bytes 458752 | tf_op jit(solution)/shard_map/stack | solution.py:24
  7.5 0.9 %copy.6 = bf16[2,28,2048]{2,0,1:T(2,128)(2,1)} copy(bf16[2,28,2048]{2,1,0:T(8,128)(2,1)S(1)} %pad_maximum_fusion) | data formatting | bytes 458752 | tf_op jit(solution)/shard_map/stack | solution.py:24
  8.5 0.0 all-gather.3.cloned.1.call-update
  8.5 7.4 %all-gather = bf16[2,28,2048]{2,1,0:T(8,128)(2,1)S(1)} all-gather(bf16[1,28,2048]{2,1,0:T(8,128)(2,1)} %bitcast.54), channel_id=1, replica_groups=mesh['blk'=16,'rep'=2] {'rep'}, dimensions={0}, use_global_device_ids=true | all-gather | bytes 344064 | tf_op jit(solution)/shard_map/all_gather | solution.py:21
  15.9 0.1 reshape.6
  16.7 0.2 fusion.9
  16.8 43.2 %all-gather.3.cloned.1.call-done = bf16[2,448,2048]{2,0,1:T(2,128)(2,1)} async-done(((bf16[2,28,2048]{2,0,1:T(2,128)(2,1)}), bf16[2,448,2048]{2,0,1:T(2,128)(2,1)}) %all-gather.3.cloned.1.call-update) | async-done | bytes 3670032 | tf_op jit(solution)/shard_map/all_gather | solution.py:25
  60.0 3.6 %copy.8 = bf16[2,448,2048]{2,1,0:T(8,128)(2,1)S(1)} copy(bf16[2,448,2048]{2,0,1:T(2,128)(2,1)} %all-gather.3.cloned.1.call-done) | data formatting | bytes 7340032 | tf_op jit(solution)/shard_map/all_gather | solution.py:25
  63.7 0.0 copy-start
  63.7 0.4 multiply_reduce_fusion
  64.1 0.8 fusion.17
  64.9 0.8 copy-done
  65.7 0.0 copy-start.1
  65.7 1.2 %convolution_bitcast_fusion = f32[2,56,2048]{2,1,0:T(8,128)S(1)} fusion(bf16[56,448]{1,0:T(8,128)(2,1)S(1)} %get-tuple-element.6, bf16[2,448,2048]{2,0,1:T(2,128)(2,1)S(1)} %copy-done), kind=kOutput, calls=%fused_computation.1 | convolution fusion | flops 205520896 | bytes 4637696 | tf_op jit(solution)/shard_map/ij,cjd->cid/dot_general | solution.py:28
  67.0 0.2 fusion.13
  67.1 11.4 %fusion = f32[32,2048]{1,0:T(8,128)S(1)} fusion(f32[56,2048]{1,0:T(8,128)S(1)} %fusion.13), kind=kCustom, calls=%all-reduce-scatter | all-reduce-scatter fusion | flops 131073 | bytes 721408
  78.5 2.5 %collective-permute-start = (f32[4,2048]{1,0:T(4,128)S(1)}, f32[4,2048]{1,0:T(4,128)S(1)}, u32[]{:S(2)}, u32[]{:S(2)}) collective-permute-start(f32[4,2048]{1,0:T(4,128)S(1)} %slice.15), channel_id=1, source_target_pairs={{0,1},{2,3},{4,5},{6,7},{8,9},{10,11},{12,13},{14,15},{16,17},{18,... | collective-permute-start | bytes 98312
  81.0 0.0 copy-done.1
  81.0 0.6 dynamic-slice.4
  82.2 0.3 collective-permute-done
  82.6 0.2 concatenate
  82.8 0.7 constant_dynamic-slice_fusion
  (1 shorter events, 0.0 us)
Async XLA Ops:
  6.5 53.5 %all-gather.3.cloned.1.call-start = ((), (), s32[]{:S(2)}) async-start(), calls=%async_computation | async-start | bytes 3899392 | tf_op jit(solution)/shard_map/all_gather | solution.py:25
  63.7 2.0 %copy-start = (bf16[2,448,2048]{2,0,1:T(2,128)(2,1)S(1)}, bf16[2,448,2048]{2,0,1:T(2,128)(2,1)}, u32[]{:S(2)}) copy-start(bf16[2,448,2048]{2,0,1:T(2,128)(2,1)} %all-gather.3.cloned.1.call-done) | copy-start | bytes 11010052
  65.7 15.3 %copy-start.1 = (u32[32]{0:T(128)S(1)}, u32[32]{0:T(128)}, u32[]{:S(2)}) copy-start(u32[32]{0:T(128)} %constant.16) | copy-start | bytes 388
  78.5 4.0 %collective-permute-start = (f32[4,2048]{1,0:T(4,128)S(1)}, f32[4,2048]{1,0:T(4,128)S(1)}, u32[]{:S(2)}, u32[]{:S(2)}) collective-permute-start(f32[4,2048]{1,0:T(4,128)S(1)} %slice.15), channel_id=1, source_target_pairs={{0,1},{2,3},{4,5},{6,7},{8,9},{10,11},{12,13},{14,15},{16,17},{18,... | collective-permute-start | bytes 98312
Sparse Core Ops, SparseCore 0:
  9.6 50.3 all-gather.2
where the time goes:
time: 90.7 us; the launch traced here: 90.4 us
  waiting for transfers between devices  43.6 us (48%)
  blocking collectives  18.8 us (21%)
  between operations  14.8 us (16%)
  local copies, waits for them, and re-layouts  7.03 us (8%)
  starting transfers between devices  2.46 us (3%)
  matrix products  2.01 us (2%)
  other arithmetic  1.75 us (2%)
    all_gather x1, waiting for transfers between devices, shards(): source = lax.all_gather(stacked, 'blk', axis=1, tiled=True)  43.2 us
    unnamed x1, blocking collectives  11.4 us
    all_gather x1, blocking collectives, shards(): targets = lax.all_gather(particles, 'rep', axis=0, tiled=True)  7.42 us
    all_gather x1, local copies, waits for them, and re-layouts, shards(): source = lax.all_gather(stacked, 'blk', axis=1, tiled=True)  3.65 us
    unnamed x9, local copies, waits for them, and re-layouts  2.46 us
    unnamed x1, starting transfers between devices  2.46 us
  transfers between devices with their start and end apart: 2, of which 2 were waited for; matrix products, arithmetic and copies ran while one was open for 1% of the time, Pallas kernels for 0%

commit v1 on v0

--- a/solution.py
+++ b/solution.py
@@ -22,7 +22,7 @@
     target_wide = targets.astype(jnp.float32)
     target_norm = jnp.sum(target_wide * target_wide, axis=1)
     stacked = jnp.stack([scores, particles], axis=0)
-    source = lax.all_gather(stacked, "blk", axis=1, tiled=True)
+    source = jnp.concatenate(lax.all_gather(stacked, "blk"), axis=1)
     weights = kernel_weights(targets, target_norm, source[1], inverse)
     weights_low = weights.astype(jnp.bfloat16)
     combined_step = jnp.einsum(

time: 90.7 us -> 104 us (1.15)
  local copies, waits for them, and re-layouts: 7.03 us -> 12.9 us
  matrix products: 2.01 us -> 5.57 us
  waiting for transfers between devices: 43.6 us -> 46.4 us
    reshape x0 -> x1, local copies, waits for them, and re-layouts: none -> 5.61 us  [shards(): source = jnp.concatenate(lax.all_gather(stacked, 'blk'), axis=1)]
    all_gather x1, waiting for transfers between devices: 43.2 us -> 46 us  [shards(): source = jnp.concatenate(lax.all_gather(stacked, 'blk'), axis=1)]
    dot_general x1, matrix products: 1.25 us -> 3.3 us  [shards(): jnp.einsum('ij,cjd->cid', weights_low, source, preferred_element_type=jnp...]
    dot_general x1, matrix products: 0.76 us -> 2.27 us  [kernel_weights(): lax.dot_general(targets, source_x, (((1,), (1,)), ((), ())), preferred_el...]
    squeeze x0 -> x1, local copies, waits for them, and re-layouts: none -> 1.43 us  [shards(): weights = kernel_weights(targets, target_norm, source[1], inverse)]
    all_gather x1, local copies, waits for them, and re-layouts: 3.65 us -> 2.49 us  [shards(): source = jnp.concatenate(lax.all_gather(stacked, 'blk'), axis=1)]
where the time goes in v1:
time: 104 us; the launch traced here: 103 us
  waiting for transfers between devices  46.4 us (45%)
  blocking collectives  18.8 us (18%)
  between operations  14.8 us (14%)
  local copies, waits for them, and re-layouts  12.9 us (12%)
  matrix products  5.57 us (5%)
  other arithmetic  2.54 us (2%)
  starting transfers between devices  2.46 us (2%)
    all_gather x1, waiting for transfers between devices, shards(): source = jnp.concatenate(lax.all_gather(stacked, 'blk'), axis=1)  46 us
    unnamed x1, blocking collectives  11.4 us
    all_gather x1, blocking collectives, shards(): targets = lax.all_gather(particles, 'rep', axis=0, tiled=True)  7.42 us
    reshape x1, local copies, waits for them, and re-layouts, shards(): source = jnp.concatenate(lax.all_gather(stacked, 'blk'), axis=1)  5.61 us
    dot_general x1, matrix products, shards(): jnp.einsum('ij,cjd->cid', weights_low, source, preferred_element_type=jnp...  3.3 us
    unnamed x9, local copies, waits for them, and re-layouts  3.15 us
    all_gather x1, local copies, waits for them, and re-layouts, shards(): source = jnp.concatenate(lax.all_gather(stacked, 'blk'), axis=1)  2.49 us
    unnamed x1, starting transfers between devices  2.46 us
  transfers between devices with their start and end apart: 2, of which 2 were waited for; matrix products, arithmetic and copies ran while one was open for 1% of the time, Pallas kernels for 0%

profile of v1, /device:TPU:0, one launch (start us, length us, event | category | flops | bytes accessed | tf_op | source)
XLA Modules:
  0.0 103.5 jit_solution(4256327304731462741)
XLA Ops:
  6.5 0.0 all-gather.4.cloned.1.call-start
  6.5 1.7 %pad_maximum_fusion = bf16[2,28,2048]{2,1,0:T(8,128)(2,1)} fusion(bf16[1,28,2048]{2,1,0:T(8,128)(2,1)} %bitcast.45, bf16[1,28,2048]{2,1,0:T(8,128)(2,1)} %bitcast.47), kind=kLoop, calls=%fused_computation.21 | loop fusion | flops 114688 | bytes 458752 | tf_op jit(solution)/shard_map/stack | solution.py:24
  8.2 0.0 all-gather.4.cloned.1.call-update
  8.3 7.4 %all-gather.1 = bf16[2,28,2048]{2,1,0:T(8,128)(2,1)S(1)} all-gather(bf16[1,28,2048]{2,1,0:T(8,128)(2,1)} %bitcast.46), channel_id=1, replica_groups=mesh['blk'=16,'rep'=2] {'rep'}, dimensions={0}, use_global_device_ids=true | all-gather | bytes 344064 | tf_op jit(solution)/shard_map/all_gather | solution.py:21
  15.7 0.1 reshape.19
  16.4 0.2 fusion.12
  16.6 46.0 %all-gather.4.cloned.1.call-done = bf16[32,28,2048]{2,1,0:T(8,128)(2,1)} async-done(((bf16[2,28,2048]{2,1,0:T(8,128)(2,1)}), bf16[32,28,2048]{2,1,0:T(8,128)(2,1)}) %all-gather.4.cloned.1.call-update) | async-done | bytes 3670032 | tf_op jit(solution)/shard_map/all_gather | solution.py:25
  62.6 2.5 %copy.17 = bf16[16,2,28,2048]{3,2,0,1:T(8,128)(2,1)S(1)} copy(bf16[16,2,28,2048]{3,2,1,0:T(8,128)(2,1)} %bitcast.42) | data formatting | bytes 7340032 | tf_op jit(solution)/shard_map/all_gather | solution.py:25
  65.1 0.0 copy-start
  65.1 0.1 slice.13
  65.3 0.5 multiply_reduce_fusion
  65.8 1.5 %copy-done = bf16[32,28,2048]{2,1,0:T(8,128)(2,1)S(1)} copy-done((bf16[32,28,2048]{2,1,0:T(8,128)(2,1)S(1)}, bf16[32,28,2048]{2,1,0:T(8,128)(2,1)}, u32[]{:S(2)}) %copy-start) | copy-done | bytes 3670040
  67.3 5.6 %copy.9 = bf16[2,16,28,2048]{3,0,2,1:T(2,128)(2,1)} copy(bf16[2,16,28,2048]{3,2,0,1:T(8,128)(2,1)S(1)} %bitcast.43) | data formatting | bytes 7340032 | tf_op jit(solution)/shard_map/reshape | solution.py:25
  72.9 1.4 %squeeze.10 = bf16[448,2048]{1,0:T(8,128)(2,1)} reshape(bf16[1,16,28,2048]{3,2,1,0:T(8,128)(2,1)S(1)} %slice.13) | data formatting | bytes 3670016 | tf_op jit(solution)/shard_map/squeeze | solution.py:26
  74.4 0.1 add.21
  74.4 2.3 %fusion.19 = (f32[56]{0:T(128)S(1)}, bf16[56,448]{1,0:T(8,128)(2,1)S(1)}) fusion(f32[]{:T(128)} %bitcast.7, bf16[448,2048]{1,0:T(8,128)(2,1)} %squeeze.10, bf16[56,2048]{1,0:T(8,128)(2,1)S(1)} %reshape.19, f32[448]{0:T(512)S(1)} %add.21, f32[56]{0:T(128)S(1)} %fusion.12), kind=kOutput, calls=%fused_computation.25 | convolution fusion | flops 102961096 | bytes 2116804 | tf_op jit(solution)/shard_map/dot_general | solution.py:8
  76.7 0.0 copy-start.1
  76.7 3.3 %fusion.3 = f32[2,56,2048]{2,1,0:T(8,128)S(1)} fusion(bf16[2,448,2048]{2,0,1:T(2,128)(2,1)} %bitcast.44, bf16[56,448]{1,0:T(8,128)(2,1)S(1)} %get-tuple-element.6), kind=kOutput, calls=%fused_computation.4 | convolution fusion | flops 205520896 | bytes 4637696 | tf_op jit(solution)/shard_map/ij,cjd->cid/dot_general | solution.py:28
  80.0 0.2 fusion.16
  80.2 11.4 %fusion = f32[32,2048]{1,0:T(8,128)S(1)} fusion(f32[56,2048]{1,0:T(8,128)S(1)} %fusion.16), kind=kCustom, calls=%all-reduce-scatter | all-reduce-scatter fusion | flops 131073 | bytes 721408
  91.6 2.5 %collective-permute-start = (f32[4,2048]{1,0:T(4,128)S(1)}, f32[4,2048]{1,0:T(4,128)S(1)}, u32[]{:S(2)}, u32[]{:S(2)}) collective-permute-start(f32[4,2048]{1,0:T(4,128)S(1)} %slice.16), channel_id=1, source_target_pairs={{0,1},{2,3},{4,5},{6,7},{8,9},{10,11},{12,13},{14,15},{16,17},{18,... | collective-permute-start | bytes 98312
  94.1 0.0 copy-done.1
  94.1 0.6 dynamic-slice.4
  95.3 0.3 collective-permute-done
  95.6 0.2 concatenate
  95.9 0.7 constant_dynamic-slice_fusion
  (1 shorter events, 0.0 us)
Async XLA Ops:
  6.5 56.1 %all-gather.4.cloned.1.call-start = ((), (), s32[]{:S(2)}) async-start(), calls=%async_computation | async-start | bytes 4456448 | tf_op jit(solution)/shard_map/all_gather | solution.py:25
  65.1 2.2 %copy-start = (bf16[32,28,2048]{2,1,0:T(8,128)(2,1)S(1)}, bf16[32,28,2048]{2,1,0:T(8,128)(2,1)}, u32[]{:S(2)}) copy-start(bf16[32,28,2048]{2,1,0:T(8,128)(2,1)} %all-gather.4.cloned.1.call-done) | copy-start | bytes 11010052
  76.7 17.3 %copy-start.1 = (u32[32]{0:T(128)S(1)}, u32[32]{0:T(128)}, u32[]{:S(2)}) copy-start(u32[32]{0:T(128)} %constant.16) | copy-start | bytes 388
  91.6 4.0 %collective-permute-start = (f32[4,2048]{1,0:T(4,128)S(1)}, f32[4,2048]{1,0:T(4,128)S(1)}, u32[]{:S(2)}, u32[]{:S(2)}) collective-permute-start(f32[4,2048]{1,0:T(4,128)S(1)} %slice.16), channel_id=1, source_target_pairs={{0,1},{2,3},{4,5},{6,7},{8,9},{10,11},{12,13},{14,15},{16,17},{18,... | collective-permute-start | bytes 98312
Sparse Core Ops, SparseCore 0:
  9.5 53.0 all-gather.3
